TPU v7x, 256 devices: a whole 4x4x8 slice. The times are simulated.
256 devices in a mesh: slab: 32 (over x, y, core), probe: 8 (over z).
Axes of the slice: x: 4, y: 4, z: 8, core: 2. Of those that a mesh axis runs over, the one named last changes fastest.
Arguments:
- probes: float32 [16, 3, 64, 128, 128], P('probe', None, 'slab'), may hold values from -50 to 50
- earlier: float32 [16, 3, 64, 128, 128], P(None, None, 'slab', 'probe'), may hold values from -16 to 16
- modulus: float32 [64, 128, 128], P('slab'), may hold values from 0.5 to 2
- tangent: float32 [6, 64, 128, 128], P(None, 'slab'), may hold values from -0.3 to 2, as said below
Outputs:
- basis: float32 [16, 3, 64, 128, 128], P('probe', None, 'slab')
- correlation: float32 [16, 16], replicated
Inputs may be any that keep to these rules, and one draw needn't show every extreme that they name: `tangent`: entries 0 to 2 lie in 1 to 2, entries 3 to 5 in -0.3 to 0.3.
All inputs are finite; a program needn't handle non-finite values.
Results may differ from a plain program's by a relative error of at most 0.00014.
Values sent between devices are 32-bit elements; how exact they have to be, the bound alone decides.
No kernel may reach another device: no remote copies, remote signals or barrier semaphores. Data moves between devices by JAX's collectives and lax.ppermute only.
A program may use at most 64 MiB of HBM per device.

v0:
```python
import jax
import jax.numpy as jnp
from jax import lax
from jax.sharding import PartitionSpec as P


def padded_2(cells, sides, width):
    for axis, dim in sides:
        count = lax.axis_size(axis)
        ends = count - 1
        head = lax.slice_in_dim(cells, 0, width, axis=dim)
        tail = lax.slice_in_dim(cells, cells.shape[dim] - width, cells.shape[dim], axis=dim)
        cells = jnp.concatenate(
            [
                lax.ppermute(tail, axis, [(i, (i + 1) % count) for i in range(ends)]),
                cells,
                lax.ppermute(head, axis, [((i + 1) % count, i) for i in range(ends)]),
            ],
            axis=dim,
        )
    return cells


def scaled_tangent(vectors, modulus, tensor):
    planes = vectors.shape[2] - 2
    height = vectors.shape[3]
    breadth = vectors.shape[4]
    padded = jnp.pad(vectors, ((0, 0), (0, 0), (0, 0), (1, 1), (1, 1)))
    mod_pad = jnp.pad(modulus, ((0, 0), (1, 1), (1, 1)))
    centre = padded[:, :, 1 : planes + 1, 1 : height + 1, 1 : breadth + 1]
    mod_centre = mod_pad[1 : planes + 1, 1 : height + 1, 1 : breadth + 1]
    summed = jnp.zeros_like(centre)
    for step_z in (-1, 0, 1):
        for step_y in (-1, 0, 1):
            for step_x in (-1, 0, 1):
                reach = abs(step_z) + abs(step_y) + abs(step_x)
                if reach == 0:
                    continue
                weight = (0.3, 0.1, 0.05)[reach - 1]
                nearby = padded[
                    :,
                    :,
                    1 + step_z : planes + 1 + step_z,
                    1 + step_y : height + 1 + step_y,
                    1 + step_x : breadth + 1 + step_x,
                ]
                mod_near = mod_pad[
                    1 + step_z : planes + 1 + step_z,
                    1 + step_y : height + 1 + step_y,
                    1 + step_x : breadth + 1 + step_x,
                ]
                edge_coef = 0.5 * weight * (mod_centre + mod_near)
                summed = summed + edge_coef * (centre - nearby)
    first_c = centre[:, 0]
    second_c = centre[:, 1]
    third_c = centre[:, 2]
    local_part = jnp.stack(
        [
            tensor[0] * first_c + tensor[3] * second_c + tensor[4] * third_c,
            tensor[3] * first_c + tensor[1] * second_c + tensor[5] * third_c,
            tensor[4] * first_c + tensor[5] * second_c + tensor[2] * third_c,
        ],
        axis=1,
    )
    return (summed + local_part - 8.0 * centre) / 8.0


def body(probes, earlier, modulus, tangent):
    depth = probes.shape[2]
    slabs = lax.axis_size("slab")
    highest = lax.Precision.HIGHEST
    ext_probe, ext_mod = (
        padded_2(probes, (("slab", 2),), 1),
        padded_2(modulus[None, None], (("slab", 2),), 1),
    )
    mod_wide = ext_mod[0, 0]
    first = scaled_tangent(ext_probe, mod_wide, tangent)
    ext_first = padded_2(first, (("slab", 2),), 1)
    second = scaled_tangent(ext_first, mod_wide, tangent)
    filtered = 2.0 * second - probes
    rows_y = lax.all_to_all(filtered, "probe", split_axis=3, concat_axis=0, tiled=True)
    flat_y = rows_y.reshape(rows_y.shape[0], -1)
    flat_q = earlier.reshape(earlier.shape[0], -1)
    scale = jnp.sqrt(jnp.float32(3 * depth * slabs * probes.shape[3] * probes.shape[4]))
    qq_part = jnp.dot(flat_q, flat_q.T, precision=highest)
    qy_part = jnp.dot(flat_q, flat_y.T, precision=highest)
    gram_earlier, cross = lax.psum((qq_part, qy_part), ("slab", "probe"))
    coeff = jax.scipy.linalg.cho_solve((jnp.linalg.cholesky(gram_earlier), True), cross)
    residue = flat_y - jnp.dot(coeff.T, flat_q, precision=highest)
    group_width = probes.shape[0]
    groups_total = lax.axis_size("probe")
    groups = [residue[k * group_width : (k + 1) * group_width] for k in range(groups_total)]
    for k in range(groups_total):
        own_group = groups[k]
        group_gram = lax.psum(jnp.dot(own_group, own_group.T, precision=highest), ("slab", "probe"))
        own_group = jax.scipy.linalg.solve_triangular(
            jnp.linalg.cholesky(group_gram), own_group, lower=True
        )
        later = groups[k + 1 :]
        if len(later) > 0:
            remaining = jnp.concatenate(later, axis=0)
            along = lax.psum(jnp.dot(remaining, own_group.T, precision=highest), ("slab", "probe"))
            remaining = remaining - jnp.dot(along, own_group, precision=highest)
            later = [remaining[m * group_width : (m + 1) * group_width] for m in range(len(later))]
        groups = groups[:k] + [own_group] + later
    basis_rows = jnp.concatenate(groups, axis=0)
    basis_rows = (basis_rows * scale).reshape(rows_y.shape)
    basis = lax.all_to_all(basis_rows, "probe", split_axis=0, concat_axis=3, tiled=True)
    return (basis, coeff * scale)


def solution(mesh):
    in_specs = (
        P("probe", None, "slab", None, None),
        P(None, None, "slab", "probe", None),
        P("slab", None, None),
        P(None, "slab", None, None),
    )
    out_specs = (P("probe", None, "slab", None, None), P())
    return jax.shard_map(body, mesh=mesh, in_specs=in_specs, out_specs=out_specs, check_vma=False)
```

profile of v0, /device:TPU:2, one launch (start us, length us, event | category | flops | bytes accessed | tf_op | source)
XLA Modules:
  0.0 1344.2 jit_solution(6016094942642158708)
XLA Ops:
  0.7 1.0 fusion.249
  1.6 1.9 collective-permute-start
  3.5 5.8 collective-permute-start.1
  9.3 1.2 fusion.248
  10.5 1.9 collective-permute-start.2
  12.4 5.8 collective-permute-start.3
  18.2 1.3 slice_bitcast_fusion.5
  19.5 1.1 multiply_add_fusion.5
  21.0 1.2 fusion.133
  22.3 1.2 collective-permute-done.3
  23.4 1.5 select_maximum_fusion.2
  24.9 5.1 broadcast_multiply_fusion.1
  30.3 1.9 collective-permute-start.4
  32.2 5.9 collective-permute-start.5
  38.1 2.2 multiply_add_fusion.2
  40.3 1.3 collective-permute-done.4
  41.7 1.8 collective-permute-done.5
  43.4 1.5 select_maximum_fusion
  44.9 5.5 fusion.10
  50.4 1.5 copy.134
  51.9 8.5 all-to-all-start
  60.4 1.4 convolution_bitcast_fusion.2
  61.8 23.6 %all-to-all-done = f32[2,3,2,128,128]{4,1,2,0,3:T(4,128)S(1)} async-done(((f32[2,3,2,128,128]{4,1,2,0,3:T(4,128)}), f32[2,3,2,128,128]{4,1,2,0,3:T(4,128)S(1)}, u32[]{:S(2)}, u32[]{:S(2)}) %all-to-all-start) | async-done | bytes 786464 | tf_op jit(solution)/shard_map/all_to_all | solution.py:81
  85.9 1.4 convolution_bitcast_fusion.1
  87.2 76.8 %all-reduce.3 = (f32[16,16]{0,1:T(8,128)S(1)}, f32[16,16]{0,1:T(8,128)S(1)}) all-reduce(f32[16,16]{0,1:T(8,128)S(1)} %convolution_bitcast_fusion.1, f32[16,16]{0,1:T(8,128)S(1)} %convolution_bitcast_fusion.2), channel_id=1, replica_groups=mesh['slab'=32,'probe'=8] {'slab','probe'}, use_global_device_ids=true, to_apply=%region_3.4 | all-reduce | flops 512 | bytes 4096 | tf_op jit(solution)/shard_map/psum | solution.py:87
  164.1 1.5 cholesky.30
  166.9 1.2 custom-call.15
  169.1 1.2 convolution_subtract_fusion
  171.2 74.2 %psum.121 = f32[2,2]{0,1:T(2,128)S(1)} all-reduce(f32[2,2]{0,1:T(2,128)S(1)} %fusion.214), channel_id=1, replica_groups=mesh['slab'=32,'probe'=8] {'slab','probe'}, use_global_device_ids=true, to_apply=%region_4.5 | all-reduce | flops 4 | bytes 32 | tf_op jit(solution)/shard_map/psum | solution.py:95
  247.8 1.0 fusion.124
  248.8 73.3 %psum.122 = f32[14,2]{0,1:T(2,128)S(1)} all-reduce(f32[14,2]{0,1:T(2,128)S(1)} %fusion.124), channel_id=1, replica_groups=mesh['slab'=32,'probe'=8] {'slab','probe'}, use_global_device_ids=true, to_apply=%region_7.10 | all-reduce | flops 28 | bytes 224 | tf_op jit(solution)/shard_map/psum | solution.py:102
  324.0 74.3 %psum.123 = f32[2,2]{0,1:T(2,128)S(1)} all-reduce(f32[2,2]{0,1:T(2,128)S(1)} %fusion.210), channel_id=1, replica_groups=mesh['slab'=32,'probe'=8] {'slab','probe'}, use_global_device_ids=true, to_apply=%region_8.11 | all-reduce | flops 4 | bytes 32 | tf_op jit(solution)/shard_map/psum | solution.py:95
  400.6 1.0 fusion.122
  401.6 73.3 %psum.124 = f32[12,2]{0,1:T(2,128)S(1)} all-reduce(f32[12,2]{0,1:T(2,128)S(1)} %fusion.122), channel_id=1, replica_groups=mesh['slab'=32,'probe'=8] {'slab','probe'}, use_global_device_ids=true, to_apply=%region_9.12 | all-reduce | flops 24 | bytes 192 | tf_op jit(solution)/shard_map/psum | solution.py:102
  476.8 74.4 %psum.125 = f32[2,2]{0,1:T(2,128)S(1)} all-reduce(f32[2,2]{0,1:T(2,128)S(1)} %fusion.206), channel_id=1, replica_groups=mesh['slab'=32,'probe'=8] {'slab','probe'}, use_global_device_ids=true, to_apply=%region_10.13 | all-reduce | flops 4 | bytes 32 | tf_op jit(solution)/shard_map/psum | solution.py:95
  553.6 1.0 fusion.120
  554.6 73.3 %psum.126 = f32[10,2]{0,1:T(2,128)S(1)} all-reduce(f32[10,2]{0,1:T(2,128)S(1)} %fusion.120), channel_id=1, replica_groups=mesh['slab'=32,'probe'=8] {'slab','probe'}, use_global_device_ids=true, to_apply=%region_11.14 | all-reduce | flops 20 | bytes 160 | tf_op jit(solution)/shard_map/psum | solution.py:102
  629.8 74.2 %psum.127 = f32[2,2]{0,1:T(2,128)S(1)} all-reduce(f32[2,2]{0,1:T(2,128)S(1)} %fusion.202), channel_id=1, replica_groups=mesh['slab'=32,'probe'=8] {'slab','probe'}, use_global_device_ids=true, to_apply=%region_12.15 | all-reduce | flops 4 | bytes 32 | tf_op jit(solution)/shard_map/psum | solution.py:95
  707.3 73.3 %psum.128 = f32[8,2]{0,1:T(2,128)S(1)} all-reduce(f32[8,2]{0,1:T(2,128)S(1)} %fusion.128), channel_id=1, replica_groups=mesh['slab'=32,'probe'=8] {'slab','probe'}, use_global_device_ids=true, to_apply=%region_13.16 | all-reduce | flops 16 | bytes 128 | tf_op jit(solution)/shard_map/psum | solution.py:102
  782.2 74.2 %psum.129 = f32[2,2]{0,1:T(2,128)S(1)} all-reduce(f32[2,2]{0,1:T(2,128)S(1)} %fusion.198), channel_id=1, replica_groups=mesh['slab'=32,'probe'=8] {'slab','probe'}, use_global_device_ids=true, to_apply=%region_14.17 | all-reduce | flops 4 | bytes 32 | tf_op jit(solution)/shard_map/psum | solution.py:95
  859.7 73.3 %psum.130 = f32[6,2]{0,1:T(2,128)S(1)} all-reduce(f32[6,2]{0,1:T(2,128)S(1)} %fusion.126), channel_id=1, replica_groups=mesh['slab'=32,'probe'=8] {'slab','probe'}, use_global_device_ids=true, to_apply=%region_15.18 | all-reduce | flops 12 | bytes 96 | tf_op jit(solution)/shard_map/psum | solution.py:102
  934.5 74.4 %psum.131 = f32[2,2]{0,1:T(2,128)S(1)} all-reduce(f32[2,2]{0,1:T(2,128)S(1)} %fusion.194), channel_id=1, replica_groups=mesh['slab'=32,'probe'=8] {'slab','probe'}, use_global_device_ids=true, to_apply=%region_16.19 | all-reduce | flops 4 | bytes 32 | tf_op jit(solution)/shard_map/psum | solution.py:95
  1012.3 73.3 %psum.132 = f32[4,2]{0,1:T(2,128)S(1)} all-reduce(f32[4,2]{0,1:T(2,128)S(1)} %fusion.130), channel_id=1, replica_groups=mesh['slab'=32,'probe'=8] {'slab','probe'}, use_global_device_ids=true, to_apply=%region_17.20 | all-reduce | flops 8 | bytes 64 | tf_op jit(solution)/shard_map/psum | solution.py:102
  1087.1 74.2 %psum.133 = f32[2,2]{0,1:T(2,128)S(1)} all-reduce(f32[2,2]{0,1:T(2,128)S(1)} %fusion.190), channel_id=1, replica_groups=mesh['slab'=32,'probe'=8] {'slab','probe'}, use_global_device_ids=true, to_apply=%region_18.21 | all-reduce | flops 4 | bytes 32 | tf_op jit(solution)/shard_map/psum | solution.py:95
  1164.7 73.3 %psum.134 = f32[2,2]{1,0:T(2,128)S(1)} all-reduce(f32[2,2]{1,0:T(2,128)S(1)} %fusion.186), channel_id=1, replica_groups=mesh['slab'=32,'probe'=8] {'slab','probe'}, use_global_device_ids=true, to_apply=%region_19.22 | all-reduce | flops 4 | bytes 32 | tf_op jit(solution)/shard_map/psum | solution.py:102
  1239.4 74.2 %psum.135 = f32[2,2]{0,1:T(2,128)S(1)} all-reduce(f32[2,2]{0,1:T(2,128)S(1)} %fusion.250), channel_id=1, replica_groups=mesh['slab'=32,'probe'=8] {'slab','probe'}, use_global_device_ids=true, to_apply=%region_20.23 | all-reduce | flops 4 | bytes 32 | tf_op jit(solution)/shard_map/psum | solution.py:95
  1316.4 26.6 %all_to_all.33 = f32[16,3,2,16,128]{4,3,2,1,0:T(8,128)S(1)} all-to-all(f32[16,3,2,16,128]{4,3,2,1,0:T(8,128)S(1)} %broadcast_multiply_fusion), channel_id=1, replica_groups=mesh['slab'=32,'probe'=8] {'probe'}, dimensions={0} | all-to-all | bytes 1572864 | tf_op jit(solution)/shard_map/all_to_all | solution.py:108
  1343.0 0.9 copy.164
  (169 shorter events, 38.4 us)
Async XLA Ops:
  0.6 20.0 %copy-start.2 = (f32[2,128,128]{2,1,0:T(8,128)S(1)}, f32[2,128,128]{2,1,0:T(8,128)}, u32[]{:S(2)}) copy-start(f32[2,128,128]{2,1,0:T(8,128)} %param.9) | copy-start | bytes 393220
  0.6 18.9 %copy-start = (f32[2,3,2,128,128]{4,3,2,1,0:T(8,128)S(1)}, f32[2,3,2,128,128]{4,3,2,1,0:T(8,128)}, u32[]{:S(2)}) copy-start(f32[2,3,2,128,128]{4,3,2,1,0:T(8,128)} %param.7) | copy-start | bytes 2359300
  1.6 19.0 %collective-permute-start = (f32[1,1,1,128,128]{4,3,2,1,0:T(8,128)S(1)}, f32[1,1,1,128,128]{4,3,2,1,0:T(8,128)S(1)}, u32[]{:S(2)}, u32[]{:S(2)}) collective-permute-start(f32[1,1,1,128,128]{4,3,2,1,0:T(8,128)S(1)} %get-tuple-element.52), channel_id=1, source_target_pairs={{0,8},{8,16},{16,24},{24,32},{32,40},{40,48},{48,56},{56,64},{64,7... | collective-permute-start | bytes 196616 | tf_op jit(solution)/shard_map/ppermute | solution.py:15
  3.5 17.1 %collective-permute-start.1 = (f32[1,1,1,128,128]{4,3,2,1,0:T(8,128)S(1)}, f32[1,1,1,128,128]{4,3,2,1,0:T(8,128)S(1)}, u32[]{:S(2)}, u32[]{:S(2)}) collective-permute-start(f32[1,1,1,128,128]{4,3,2,1,0:T(8,128)S(1)} %get-tuple-element.53), channel_id=1, source_target_pairs={{8,0},{16,8},{24,16},{32,24},{40,32},{48,40},{56,48},{64,56},{72,6... | collective-permute-start | bytes 196616 | tf_op jit(solution)/shard_map/ppermute | solution.py:17
  10.5 11.8 collective-permute-start.2
  12.4 11.0 collective-permute-start.3
  19.4 1.2 copy-start.21
  19.4 1.2 copy-start.22
  19.5 1.2 copy-start.23
  19.5 1.2 copy-start.24
  19.5 1.2 copy-start.25
  19.5 1.2 copy-start.26
  21.0 9.1 copy-start.3
  22.1 7.9 copy-start.4
  22.1 7.9 copy-start.5
  22.1 7.9 copy-start.6
  22.1 7.9 copy-start.7
  22.1 7.9 copy-start.8
  22.1 7.9 copy-start.9
  22.2 7.9 copy-start.10
  22.2 7.9 copy-start.11
  22.2 7.9 copy-start.12
  22.2 7.9 copy-start.13
  22.2 7.9 copy-start.14
  22.2 7.9 copy-start.15
  22.2 7.9 copy-start.16
  22.2 7.9 copy-start.17
  22.2 7.9 copy-start.18
  22.2 7.9 copy-start.19
  22.3 7.9 copy-start.20
  30.3 11.4 collective-permute-start.4
  32.2 11.2 collective-permute-start.5
  50.4 10.0 copy-start.1
  51.9 33.5 %all-to-all-start = ((f32[2,3,2,128,128]{4,1,2,0,3:T(4,128)}), f32[2,3,2,128,128]{4,1,2,0,3:T(4,128)S(1)}, u32[]{:S(2)}, u32[]{:S(2)}) async-start(f32[2,3,2,128,128]{4,1,2,0,3:T(4,128)} %copy.134), calls=%async_computation | async-start | bytes 2097152 | tf_op jit(solution)/shard_map/all_to_all | solution.py:81
where the time goes:
time: 1360 us; the launch traced here: 1340 us
  blocking collectives  1210 us (89%)
  other arithmetic  36 us (3%)
  starting transfers between devices  31.7 us (2%)
  matrix products  28.7 us (2%)
  waiting for transfers between devices  27.9 us (2%)
    psum x8, blocking collectives, body(): lax.psum(jnp.dot(own_group, own_group.T, precision=highest), ('slab', 'pr...  594 us
    psum x7, blocking collectives, body(): lax.psum(jnp.dot(remaining, own_group.T, precision=highest), ('slab', 'pr...  513 us
    psum x1, blocking collectives, body(): gram_earlier, cross = lax.psum((qq_part, qy_part), ('slab', 'probe'))  76.8 us
  transfers between devices with their start and end apart: 7, of which 4 were waited for; matrix products, arithmetic and copies ran while one was open for 1% of the time, Pallas kernels for 0%

commit v1 on v0

--- a/solution.py
+++ b/solution.py
@@ -99,7 +99,12 @@
         later = groups[k + 1 :]
         if len(later) > 0:
             remaining = jnp.concatenate(later, axis=0)
-            along = lax.psum(jnp.dot(remaining, own_group.T, precision=highest), ("slab", "probe"))
+            along = jnp.sum(
+                lax.all_gather(
+                    jnp.dot(remaining, own_group.T, precision=highest), ("slab", "probe")
+                ),
+                axis=0,
+            )
             remaining = remaining - jnp.dot(along, own_group, precision=highest)
             later = [remaining[m * group_width : (m + 1) * group_width] for m in range(len(later))]
         groups = groups[:k] + [own_group] + later

time: 1360 us -> 1270 us (0.934)
  blocking collectives: 1210 us -> 1120 us
    psum x7 -> x0, blocking collectives: 513 us -> none  [body(): lax.psum(jnp.dot(remaining, own_group.T, precision=highest), ('slab', 'pr...]
    all_gather x0 -> x7, blocking collectives: none -> 440 us  [body(): lax.all_gather(jnp.dot(remaining, own_group.T, precision=highest), ('slab...]
where the time goes in v1:
time: 1270 us; the launch traced here: 1260 us
  blocking collectives  1120 us (88%)
  other arithmetic  37.9 us (3%)
  starting transfers between devices  31.7 us (2%)
  matrix products  28.7 us (2%)
  waiting for transfers between devices  27.9 us (2%)
    psum x8, blocking collectives, body(): lax.psum(jnp.dot(own_group, own_group.T, precision=highest), ('slab', 'pr...  581 us
    all_gather x7, blocking collectives, body(): lax.all_gather(jnp.dot(remaining, own_group.T, precision=highest), ('slab...  440 us
    psum x1, blocking collectives, body(): gram_earlier, cross = lax.psum((qq_part, qy_part), ('slab', 'probe'))  76.8 us
    all_to_all x1, blocking collectives, body(): lax.all_to_all(basis_rows, 'probe', split_axis=0, concat_axis=3, tiled=True)  26.5 us
  transfers between devices with their start and end apart: 7, of which 4 were waited for; matrix products, arithmetic and copies ran while one was open for 1% of the time, Pallas kernels for 0%

profile of v1, /device:TPU:2, one launch (start us, length us, event | category | flops | bytes accessed | tf_op | source)
XLA Modules:
  0.0 1259.8 jit_solution(4784023116080931405)
XLA Ops:
  0.7 1.0 fusion.242
  1.6 1.9 collective-permute-start
  3.5 5.8 collective-permute-start.1
  9.3 1.2 fusion.241
  10.5 1.9 collective-permute-start.2
  12.4 5.8 collective-permute-start.3
  18.2 1.3 slice_bitcast_fusion.5
  19.5 1.1 multiply_add_fusion.5
  21.0 1.2 fusion.127
  22.3 1.2 collective-permute-done.3
  23.4 1.5 select_maximum_fusion.2
  24.9 5.1 broadcast_multiply_fusion.1
  30.3 1.9 collective-permute-start.4
  32.2 5.9 collective-permute-start.5
  38.1 2.2 multiply_add_fusion.2
  40.3 1.3 collective-permute-done.4
  41.7 1.8 collective-permute-done.5
  43.4 1.5 select_maximum_fusion
  44.9 5.5 fusion.10
  50.4 1.5 copy.134
  51.9 8.5 all-to-all-start
  60.4 1.4 convolution_bitcast_fusion.2
  61.8 23.6 %all-to-all-done = f32[2,3,2,128,128]{4,1,2,0,3:T(4,128)S(1)} async-done(((f32[2,3,2,128,128]{4,1,2,0,3:T(4,128)}), f32[2,3,2,128,128]{4,1,2,0,3:T(4,128)S(1)}, u32[]{:S(2)}, u32[]{:S(2)}) %all-to-all-start) | async-done | bytes 786464 | tf_op jit(solution)/shard_map/all_to_all | solution.py:81
  85.9 1.4 convolution_bitcast_fusion.1
  87.2 76.8 %all-reduce.3 = (f32[16,16]{0,1:T(8,128)S(1)}, f32[16,16]{0,1:T(8,128)S(1)}) all-reduce(f32[16,16]{0,1:T(8,128)S(1)} %convolution_bitcast_fusion.1, f32[16,16]{0,1:T(8,128)S(1)} %convolution_bitcast_fusion.2), channel_id=1, replica_groups=mesh['slab'=32,'probe'=8] {'slab','probe'}, use_global_device_ids=true, to_apply=%region_3.4 | all-reduce | flops 512 | bytes 4096 | tf_op jit(solution)/shard_map/psum | solution.py:87
  164.1 1.5 cholesky.30
  166.9 1.2 custom-call.15
  169.1 1.2 convolution_subtract_fusion
  171.2 74.2 %psum.72 = f32[2,2]{0,1:T(2,128)S(1)} all-reduce(f32[2,2]{0,1:T(2,128)S(1)} %fusion.207), channel_id=1, replica_groups=mesh['slab'=32,'probe'=8] {'slab','probe'}, use_global_device_ids=true, to_apply=%region_4.5 | all-reduce | flops 4 | bytes 32 | tf_op jit(solution)/shard_map/psum | solution.py:95
  247.8 1.0 convolution_bitcast_fusion.5
  248.8 61.7 %all-gather.7 = f32[256,14,2]{1,2,0:T(2,128)S(1)} all-gather(f32[1,14,2]{1,2,0:T(2,128)S(1)} %convolution_bitcast_fusion.5), channel_id=2, replica_groups=mesh['slab'=32,'probe'=8] {'slab','probe'}, dimensions={0}, use_global_device_ids=true | all-gather | bytes 28784 | tf_op jit(solution)/shard_map/all_gather | solution.py:103
  312.7 73.3 %psum.73 = f32[2,2]{0,1:T(2,128)S(1)} all-reduce(f32[2,2]{0,1:T(2,128)S(1)} %fusion.203), channel_id=1, replica_groups=mesh['slab'=32,'probe'=8] {'slab','probe'}, use_global_device_ids=true, to_apply=%region_8.11 | all-reduce | flops 4 | bytes 32 | tf_op jit(solution)/shard_map/psum | solution.py:95
  388.3 1.0 convolution_bitcast_fusion.4
  389.4 62.0 %all-gather.8 = f32[256,12,2]{1,2,0:T(2,128)S(1)} all-gather(f32[1,12,2]{1,2,0:T(2,128)S(1)} %convolution_bitcast_fusion.4), channel_id=3, replica_groups=mesh['slab'=32,'probe'=8] {'slab','probe'}, dimensions={0}, use_global_device_ids=true | all-gather | bytes 24672 | tf_op jit(solution)/shard_map/all_gather | solution.py:103
  453.5 73.2 %psum.74 = f32[2,2]{0,1:T(2,128)S(1)} all-reduce(f32[2,2]{0,1:T(2,128)S(1)} %fusion.199), channel_id=1, replica_groups=mesh['slab'=32,'probe'=8] {'slab','probe'}, use_global_device_ids=true, to_apply=%region_10.13 | all-reduce | flops 4 | bytes 32 | tf_op jit(solution)/shard_map/psum | solution.py:95
  529.1 1.0 convolution_bitcast_fusion.3
  530.1 62.3 %all-gather.9 = f32[256,10,2]{1,2,0:T(2,128)S(1)} all-gather(f32[1,10,2]{1,2,0:T(2,128)S(1)} %convolution_bitcast_fusion.3), channel_id=4, replica_groups=mesh['slab'=32,'probe'=8] {'slab','probe'}, dimensions={0}, use_global_device_ids=true | all-gather | bytes 20560 | tf_op jit(solution)/shard_map/all_gather | solution.py:103
  594.5 72.7 %psum.75 = f32[2,2]{0,1:T(2,128)S(1)} all-reduce(f32[2,2]{0,1:T(2,128)S(1)} %fusion.195), channel_id=1, replica_groups=mesh['slab'=32,'probe'=8] {'slab','probe'}, use_global_device_ids=true, to_apply=%region_12.15 | all-reduce | flops 4 | bytes 32 | tf_op jit(solution)/shard_map/psum | solution.py:95
  670.6 63.0 %all-gather.10 = f32[256,8,2]{1,2,0:T(2,128)S(1)} all-gather(f32[1,8,2]{1,2,0:T(2,128)S(1)} %convolution_bitcast_fusion.9), channel_id=5, replica_groups=mesh['slab'=32,'probe'=8] {'slab','probe'}, dimensions={0}, use_global_device_ids=true | all-gather | bytes 16448 | tf_op jit(solution)/shard_map/all_gather | solution.py:103
  735.3 72.0 %psum.76 = f32[2,2]{0,1:T(2,128)S(1)} all-reduce(f32[2,2]{0,1:T(2,128)S(1)} %fusion.191), channel_id=1, replica_groups=mesh['slab'=32,'probe'=8] {'slab','probe'}, use_global_device_ids=true, to_apply=%region_14.17 | all-reduce | flops 4 | bytes 32 | tf_op jit(solution)/shard_map/psum | solution.py:95
  810.7 63.5 %all-gather.11 = f32[256,6,2]{1,2,0:T(2,128)S(1)} all-gather(f32[1,6,2]{1,2,0:T(2,128)S(1)} %convolution_bitcast_fusion.8), channel_id=6, replica_groups=mesh['slab'=32,'probe'=8] {'slab','probe'}, dimensions={0}, use_global_device_ids=true | all-gather | bytes 12336 | tf_op jit(solution)/shard_map/all_gather | solution.py:103
  876.0 72.0 %psum.77 = f32[2,2]{0,1:T(2,128)S(1)} all-reduce(f32[2,2]{0,1:T(2,128)S(1)} %fusion.187), channel_id=1, replica_groups=mesh['slab'=32,'probe'=8] {'slab','probe'}, use_global_device_ids=true, to_apply=%region_16.19 | all-reduce | flops 4 | bytes 32 | tf_op jit(solution)/shard_map/psum | solution.py:95
  951.3 63.7 %all-gather.12 = f32[256,4,2]{1,2,0:T(2,128)S(1)} all-gather(f32[1,4,2]{1,2,0:T(2,128)S(1)} %convolution_bitcast_fusion.7), channel_id=7, replica_groups=mesh['slab'=32,'probe'=8] {'slab','probe'}, dimensions={0}, use_global_device_ids=true | all-gather | bytes 8224 | tf_op jit(solution)/shard_map/all_gather | solution.py:103
  1016.7 71.8 %psum.78 = f32[2,2]{0,1:T(2,128)S(1)} all-reduce(f32[2,2]{0,1:T(2,128)S(1)} %fusion.183), channel_id=1, replica_groups=mesh['slab'=32,'probe'=8] {'slab','probe'}, use_global_device_ids=true, to_apply=%region_18.21 | all-reduce | flops 4 | bytes 32 | tf_op jit(solution)/shard_map/psum | solution.py:95
  1091.9 64.0 %all-gather.13 = f32[256,2,2]{2,1,0:T(2,128)S(1)} all-gather(f32[1,2,2]{2,1,0:T(2,128)S(1)} %convolution_bitcast_fusion.6), channel_id=8, replica_groups=mesh['slab'=32,'probe'=8] {'slab','probe'}, dimensions={0}, use_global_device_ids=true | all-gather | bytes 4112 | tf_op jit(solution)/shard_map/all_gather | solution.py:103
  1157.6 71.8 %psum.79 = f32[2,2]{0,1:T(2,128)S(1)} all-reduce(f32[2,2]{0,1:T(2,128)S(1)} %fusion.243), channel_id=1, replica_groups=mesh['slab'=32,'probe'=8] {'slab','probe'}, use_global_device_ids=true, to_apply=%region_20.23 | all-reduce | flops 4 | bytes 32 | tf_op jit(solution)/shard_map/psum | solution.py:95
  1232.1 26.5 %all_to_all.33 = f32[16,3,2,16,128]{4,3,2,1,0:T(8,128)S(1)} all-to-all(f32[16,3,2,16,128]{4,3,2,1,0:T(8,128)S(1)} %broadcast_multiply_fusion), channel_id=1, replica_groups=mesh['slab'=32,'probe'=8] {'probe'}, dimensions={0} | all-to-all | bytes 1572864 | tf_op jit(solution)/shard_map/all_to_all | solution.py:113
  1258.7 0.9 copy.164
  (176 shorter events, 40.3 us)
Async XLA Ops:
  0.6 20.0 %copy-start.2 = (f32[2,128,128]{2,1,0:T(8,128)S(1)}, f32[2,128,128]{2,1,0:T(8,128)}, u32[]{:S(2)}) copy-start(f32[2,128,128]{2,1,0:T(8,128)} %param.9) | copy-start | bytes 393220
  0.6 18.9 %copy-start = (f32[2,3,2,128,128]{4,3,2,1,0:T(8,128)S(1)}, f32[2,3,2,128,128]{4,3,2,1,0:T(8,128)}, u32[]{:S(2)}) copy-start(f32[2,3,2,128,128]{4,3,2,1,0:T(8,128)} %param.7) | copy-start | bytes 2359300
  1.6 19.0 %collective-permute-start = (f32[1,1,1,128,128]{4,3,2,1,0:T(8,128)S(1)}, f32[1,1,1,128,128]{4,3,2,1,0:T(8,128)S(1)}, u32[]{:S(2)}, u32[]{:S(2)}) collective-permute-start(f32[1,1,1,128,128]{4,3,2,1,0:T(8,128)S(1)} %get-tuple-element.52), channel_id=1, source_target_pairs={{0,8},{8,16},{16,24},{24,32},{32,40},{40,48},{48,56},{56,64},{64,7... | collective-permute-start | bytes 196616 | tf_op jit(solution)/shard_map/ppermute | solution.py:15
  3.5 17.1 %collective-permute-start.1 = (f32[1,1,1,128,128]{4,3,2,1,0:T(8,128)S(1)}, f32[1,1,1,128,128]{4,3,2,1,0:T(8,128)S(1)}, u32[]{:S(2)}, u32[]{:S(2)}) collective-permute-start(f32[1,1,1,128,128]{4,3,2,1,0:T(8,128)S(1)} %get-tuple-element.53), channel_id=1, source_target_pairs={{8,0},{16,8},{24,16},{32,24},{40,32},{48,40},{56,48},{64,56},{72,6... | collective-permute-start | bytes 196616 | tf_op jit(solution)/shard_map/ppermute | solution.py:17
  10.5 11.8 collective-permute-start.2
  12.4 11.0 collective-permute-start.3
  19.4 1.2 copy-start.21
  19.4 1.2 copy-start.22
  19.5 1.2 copy-start.23
  19.5 1.2 copy-start.24
  19.5 1.2 copy-start.25
  19.5 1.2 copy-start.26
  21.0 9.1 copy-start.3
  22.1 7.9 copy-start.4
  22.1 7.9 copy-start.5
  22.1 7.9 copy-start.6
  22.1 7.9 copy-start.7
  22.1 7.9 copy-start.8
  22.1 7.9 copy-start.9
  22.2 7.9 copy-start.10
  22.2 7.9 copy-start.11
  22.2 7.9 copy-start.12
  22.2 7.9 copy-start.13
  22.2 7.9 copy-start.14
  22.2 7.9 copy-start.15
  22.2 7.9 copy-start.16
  22.2 7.9 copy-start.17
  22.2 7.9 copy-start.18
  22.2 7.9 copy-start.19
  22.3 7.9 copy-start.20
  30.3 11.4 collective-permute-start.4
  32.2 11.2 collective-permute-start.5
  50.4 10.0 copy-start.1
  51.9 33.5 %all-to-all-start = ((f32[2,3,2,128,128]{4,1,2,0,3:T(4,128)}), f32[2,3,2,128,128]{4,1,2,0,3:T(4,128)S(1)}, u32[]{:S(2)}, u32[]{:S(2)}) async-start(f32[2,3,2,128,128]{4,1,2,0,3:T(4,128)} %copy.134), calls=%async_computation | async-start | bytes 2097152 | tf_op jit(solution)/shard_map/all_to_all | solution.py:81
